TPU v7x, 32 devices: a whole 2x2x4 slice. The times are simulated.
32 devices in a mesh: chan: 8 (over z, y), slot: 4 (over x, core).
Axes of the slice: x: 2, y: 2, z: 4, core: 2. Of those that a mesh axis runs over, the one named last changes fastest.
Arguments:
- visibility: float32 [2, 2, 32, 4, 3844], P(None, None, 'chan', 'slot'), parts along dimension 3, may hold values from -6 to 6
- coherency: bfloat16 [2, 2, 16, 32, 4, 3844], P(None, None, None, 'chan', 'slot'), parts along dimension 4, may hold values from -2 to 2
- jones_start: float32 [2, 2, 64, 32, 62], P(None, None, 'slot', 'chan'), parts along dimension 2, may hold values from -4 to 4
- duals_start: float32 [2, 2, 64, 32, 62], P(None, None, 'slot', 'chan'), parts along dimension 2, may hold values from -2 to 2
Outputs:
- jones_final: float32 [2, 2, 64, 32, 62], P(None, None, 'slot', 'chan'), parts along dimension 2
- consensus: float32 [2, 2, 64, 32, 62], P(None, None, 'slot', 'chan'), parts along dimension 2
- duals_final: float32 [2, 2, 64, 32, 62], P(None, None, 'slot', 'chan'), parts along dimension 2
- norms: float32 [8, 2], P('slot'), parts along dimension 0
There are 4 independent parts, one for each index of `slot`. A program takes and returns all parts, laid end to end along the dimension named above; each array names one. Nothing has to cross between parts.
All inputs are finite; a program needn't handle non-finite values.
Results may differ from a plain program's by a relative error of at most 0.0003.
Values sent between devices are 32-bit elements; how exact they have to be, the bound alone decides.
A program may use at most 128 MiB of HBM per device.

v0:
```python
import jax
import jax.numpy as jnp
from jax import lax
from jax.sharding import PartitionSpec as P

ITERS = 2


penalty = 8.0
kernel_taps = (0.04, 0.06, 0.1, 0.15, 0.3, 0.15, 0.1, 0.06, 0.04)


def padded_2(block, sides, width):
    for axis, dim in sides:
        count = lax.axis_size(axis)
        forward = [(i, i + 1) for i in range(count - 1)]
        backward = [(target, source) for source, target in forward]
        low = lax.ppermute(
            lax.slice_in_dim(block, block.shape[dim] - width, None, axis=dim), axis, forward
        )
        high = lax.ppermute(lax.slice_in_dim(block, 0, width, axis=dim), axis, backward)
        block = jnp.concatenate([low, block, high], axis=dim)
    return block


def jones_update(visibility, coherency, jones_now, target):
    width = jones_now.shape[-1]
    grid_shape = coherency.shape[1:5] + (width, width)
    sky_real = coherency[0].astype(jnp.float32).reshape(grid_shape)
    sky_imag = coherency[1].astype(jnp.float32).reshape(grid_shape)
    vis_shape = visibility.shape[1:4] + (width, width)
    data_real = visibility[0].reshape(vis_shape)[:, None]
    data_imag = visibility[1].reshape(vis_shape)[:, None]
    left_real = jones_now[0][:, :, :, None, :, None]
    left_imag = jones_now[1][:, :, :, None, :, None]
    right_real = jones_now[0][:, :, :, None, None, :]
    right_imag = jones_now[1][:, :, :, None, None, :]
    crossed = 1.0 - jnp.eye(width, dtype=jnp.float32)
    half_real = left_real * sky_real - left_imag * sky_imag
    half_imag = left_real * sky_imag + left_imag * sky_real
    model_real = half_real * right_real + half_imag * right_imag
    model_imag = half_imag * right_real - half_real * right_imag
    rest_real = (data_real - jnp.sum(model_real, axis=1, keepdims=True) + model_real) * crossed
    rest_imag = (data_imag - jnp.sum(model_imag, axis=1, keepdims=True) + model_imag) * crossed
    weight_real = sky_real * right_real + sky_imag * right_imag
    weight_imag = sky_real * right_imag - sky_imag * right_real
    upper_real = jnp.sum(rest_real * weight_real - rest_imag * weight_imag, axis=(3, 5))
    upper_imag = jnp.sum(rest_real * weight_imag + rest_imag * weight_real, axis=(3, 5))
    lower = (
        jnp.sum(
            crossed
            * (sky_real * sky_real + sky_imag * sky_imag)
            * (right_real * right_real + right_imag * right_imag),
            axis=(3, 5),
        )
        + penalty
    )
    return jnp.stack(
        [(upper_real + penalty * target[0]) / lower, (upper_imag + penalty * target[1]) / lower]
    )


def smooth(padded, channels):
    total = kernel_taps[0] * padded[:, :, :, 0:channels]
    for offset in range(1, 9):
        total = total + kernel_taps[offset] * padded[:, :, :, offset : offset + channels]
    return total


def local(visibility, coherency, jones_start, duals_start):
    channels = jones_start.shape[3]
    entries = jones_start.size * lax.axis_size("chan")
    jones_now = jones_start
    consensus = jones_start
    duals_now = duals_start
    partials = []
    for iteration in range(ITERS):
        jones_now = jones_update(visibility, coherency, jones_now, consensus - duals_now)
        padded = padded_2(jones_now + duals_now, (("chan", 3),), 4)
        fresh = smooth(padded, channels)
        duals_now = duals_now + jones_now - fresh
        primal_gap = jones_now - fresh
        moved = fresh - consensus
        pieces = (jnp.sum(primal_gap * primal_gap), penalty * penalty * jnp.sum(moved * moved))
        primal, change = lax.psum((pieces[0], pieces[1]), "chan")
        partials.append(jnp.stack([primal / entries, change / entries]))
        consensus = fresh
    norms = jnp.stack(partials)
    return (jones_now, consensus, duals_now, norms)


def solution(mesh):
    placed = (
        P(None, None, "chan", "slot", None),
        P(None, None, None, "chan", "slot", None),
        P(None, None, "slot", "chan", None),
        P(None, None, "slot", "chan", None),
    )
    return jax.shard_map(
        local,
        mesh=mesh,
        in_specs=placed,
        out_specs=(
            P(None, None, "slot", "chan", None),
            P(None, None, "slot", "chan", None),
            P(None, None, "slot", "chan", None),
            P("slot", None),
        ),
        check_vma=False,
    )
```

profile of v0, /device:TPU:0, one launch (start us, length us, event | category | flops | bytes accessed | tf_op | source)
XLA Modules:
  0.0 162.1 jit_solution(4641758411575946287)
XLA Ops:
  3.1 2.5 %mul.1257 = f32[2,16,4,62,62]{4,3,1,2,0:T(8,128)} broadcast(f32[2,16,4,62]{3,1,2,0:T(8,128)S(1)} %copy.28), dimensions={0,1,2,3} | broadcast | bytes 1999872 | tf_op jit(solution)/shard_map/mul | solution.py:39
  5.6 5.0 %mul.1258 = f32[1,2,16,4,1,3844]{5,2,3,1,4,0:T(8,128)} reshape(f32[2,16,4,62,62]{4,3,1,2,0:T(8,128)} %mul.1257) | data formatting | bytes 3936256 | tf_op jit(solution)/shard_map/mul | solution.py:39
  10.6 2.5 %mul.1261 = f32[2,16,4,62,62]{4,3,1,2,0:T(8,128)} broadcast(f32[2,16,4,62]{3,1,2,0:T(8,128)S(1)} %copy.30), dimensions={0,1,2,3} | broadcast | bytes 1999872 | tf_op jit(solution)/shard_map/mul | solution.py:39
  13.1 5.0 %mul.1262 = f32[1,2,16,4,1,3844]{5,2,3,1,4,0:T(8,128)} reshape(f32[2,16,4,62,62]{4,3,1,2,0:T(8,128)} %mul.1261) | data formatting | bytes 3936256 | tf_op jit(solution)/shard_map/mul | solution.py:39
  20.3 5.0 %mul.1265 = f32[1,2,16,4,1,3844]{5,2,3,1,4,0:T(8,128)} reshape(f32[2,16,4,62,62]{4,3,1,2,0:T(8,128)} %mul.1264) | data formatting | bytes 3936256 | tf_op jit(solution)/shard_map/mul | solution.py:41
  27.5 5.0 %mul.1270 = f32[1,2,16,4,1,3844]{5,2,3,1,4,0:T(8,128)} reshape(f32[2,16,4,62,62]{4,3,1,2,0:T(8,128)} %mul.1269) | data formatting | bytes 3936256 | tf_op jit(solution)/shard_map/mul | solution.py:41
  32.5 2.4 %fusion.49 = (bf16[1,2,16,4,1,3844]{5,3,4,2,1,0:T(4,128)(2,1)S(1)}, bf16[1,2,16,4,1,3844]{5,3,4,2,1,0:T(4,128)(2,1)S(1)}) fusion(bf16[2,2,16,4,1,3844]{5,3,4,2,1,0:T(4,128)(2,1)} %param.5), kind=kLoop, calls=%fused_computation.122 | loop fusion | bytes 3936256 | tf_op jit(solution)/shard_map/slice | solution.py:29
  34.9 2.3 %copy_convert_fusion = (f32[1,2,16,4,1,3844]{5,2,3,1,4,0:T(8,128)}, f32[1,2,16,4,1,3844]{5,2,3,1,4,0:T(8,128)}) fusion(bf16[1,2,16,4,1,3844]{5,3,4,2,1,0:T(4,128)(2,1)S(1)} %get-tuple-element.36, bf16[1,2,16,4,1,3844]{5,3,4,2,1,0:T(4,128)(2,1)S(1)} %get-tuple-element.35), kind=kLoop, calls=%fused_computation.27 | loop fusion | flops 984064 | bytes 5904384 | tf_op jit(solution)/shard_map/convert_element_type | solution.py:30
  41.0 8.4 %reshape.965 = f32[2,16,4,1,62,62]{5,4,1,2,0,3:T(8,128)} reshape(f32[1,2,16,4,1,3844]{5,2,3,1,4,0:T(8,128)} %get-tuple-element.45) | data formatting | bytes 3936256 | tf_op jit(solution)/shard_map/convert_element_type | solution.py:29
  49.4 8.2 %reshape.966 = f32[2,16,4,1,62,62]{5,4,1,2,0,3:T(8,128)} reshape(f32[1,2,16,4,1,3844]{5,2,3,1,4,0:T(8,128)} %get-tuple-element.44) | data formatting | bytes 3936256 | tf_op jit(solution)/shard_map/convert_element_type | solution.py:30
  58.5 10.0 %subtract_reduce_fusion.1 = (f32[2,16,4,62]{3,1,2,0:T(8,128)S(1)}, f32[2,16,4,62]{3,1,2,0:T(8,128)S(1)}, f32[2,16,4,62]{3,1,2,0:T(8,128)S(1)}) fusion(f32[2,16,4,1,62,62]{5,4,1,2,0,3:T(8,128)} %reshape.966, f32[2,16,4,62]{3,1,2,0:T(8,128)S(1)} %copy.30, f32[2,16,4,1,62,62]{5,4,1,2,0,3:T(8,128)} %reshape.965, f32[2,16,4,62]{3,1,2,0:T(8,128)S(1)} %copy.28, ...), kind=kLoop, calls=%fused_computation.12 | loop fusion | flops 17689344 | bytes 4388112 | tf_op jit(solution)/shard_map/reduce_sum | solution.py:47
  68.6 5.6 %collective-permute-start = (f32[2,2,16,4,62]{4,2,3,1,0:T(8,128)S(1)}, f32[2,2,16,4,62]{4,2,3,1,0:T(8,128)}, u32[]{:S(2)}, u32[]{:S(2)}) collective-permute-start(f32[2,2,16,4,62]{4,2,3,1,0:T(8,128)S(1)} %copy_add_fusion), channel_id=1, source_target_pairs={{0,4},{4,8},{8,12},{12,16},{16,20},{20,24},{24,28},{1,5},{5,9},{9,... | collective-permute-start | bytes 190472 | tf_op jit(solution)/shard_map/ppermute | solution.py:18
  75.5 2.6 %mul.1304 = f32[2,16,4,62,62]{4,3,1,2,0:T(8,128)} broadcast(f32[2,16,4,62]{3,1,2,0:T(8,128)S(1)} %get-tuple-element.30), dimensions={0,1,2,3} | broadcast | bytes 1999872 | tf_op jit(solution)/shard_map/mul | solution.py:39
  78.1 5.0 %mul.1305 = f32[1,2,16,4,1,3844]{5,2,3,1,4,0:T(8,128)} reshape(f32[2,16,4,62,62]{4,3,1,2,0:T(8,128)} %mul.1304) | data formatting | bytes 3936256 | tf_op jit(solution)/shard_map/mul | solution.py:39
  83.0 2.6 %mul.1311 = f32[2,16,4,62,62]{4,3,1,2,0:T(8,128)} broadcast(f32[2,16,4,62]{3,1,2,0:T(8,128)S(1)} %get-tuple-element.31), dimensions={0,1,2,3} | broadcast | bytes 1999872 | tf_op jit(solution)/shard_map/mul | solution.py:39
  85.6 5.0 %mul.1312 = f32[1,2,16,4,1,3844]{5,2,3,1,4,0:T(8,128)} reshape(f32[2,16,4,62,62]{4,3,1,2,0:T(8,128)} %mul.1311) | data formatting | bytes 3936256 | tf_op jit(solution)/shard_map/mul | solution.py:39
  90.6 2.2 %mul.1314 = f32[2,16,4,62,62]{4,3,1,2,0:T(8,128)} broadcast(f32[2,16,4,62]{3,1,2,0:T(8,128)S(1)} %get-tuple-element.30), dimensions={0,1,2,4} | broadcast | bytes 1999872 | tf_op jit(solution)/shard_map/mul | solution.py:41
  92.9 5.0 %mul.1315 = f32[1,2,16,4,1,3844]{5,2,3,1,4,0:T(8,128)} reshape(f32[2,16,4,62,62]{4,3,1,2,0:T(8,128)} %mul.1314) | data formatting | bytes 3936256 | tf_op jit(solution)/shard_map/mul | solution.py:41
  100.1 5.0 %mul.1320 = f32[1,2,16,4,1,3844]{5,2,3,1,4,0:T(8,128)} reshape(f32[2,16,4,62,62]{4,3,1,2,0:T(8,128)} %mul.1319) | data formatting | bytes 3936256 | tf_op jit(solution)/shard_map/mul | solution.py:41
  105.1 4.9 %subtract_reduce_fusion.2 = (f32[2,4,3844]{2,1,0:T(4,128)S(1)}, f32[2,4,3844]{2,1,0:T(4,128)S(1)}) fusion(f32[1,2,16,4,1,3844]{5,2,3,1,4,0:T(8,128)} %mul.1320, f32[1,2,16,4,1,3844]{5,2,3,1,4,0:T(8,128)} %mul.1315, f32[1,2,16,4,1,3844]{5,2,3,1,4,0:T(8,128)} %mul.1312, bf16[1,2,16,4,1,3844]{5,3,4,2,1,0:T(4,128)(2,1)S(1)} %get-tuple-element.36, ...), kind=kLoop, calls=%fused_computation.19 | loop fusion | flops 7811008 | bytes 10086656 | tf_op jit(solution)/shard_map/reduce_sum | solution.py:44
  110.8 10.0 %subtract_reduce_fusion = (f32[2,16,4,62]{3,1,2,0:T(8,128)S(1)}, f32[2,16,4,62]{3,1,2,0:T(8,128)S(1)}, f32[2,16,4,62]{3,1,2,0:T(8,128)S(1)}) fusion(f32[2,16,4,1,62,62]{5,4,1,2,0,3:T(8,128)} %reshape.966, f32[2,16,4,62]{3,1,2,0:T(8,128)S(1)} %get-tuple-element.31, f32[2,16,4,1,62,62]{5,4,1,2,0,3:T(8,128)} %reshape.965, ...), kind=kLoop, calls=%fused_computation.2 | loop fusion | flops 17689344 | bytes 4388112 | tf_op jit(solution)/shard_map/reduce_sum | solution.py:47
  122.1 4.6 %collective-permute-start.2 = (f32[2,2,16,4,62]{4,2,3,1,0:T(8,128)S(1)}, f32[2,2,16,4,62]{4,2,3,1,0:T(8,128)S(1)}, u32[]{:S(2)}, u32[]{:S(2)}) collective-permute-start(f32[2,2,16,4,62]{4,2,3,1,0:T(8,128)S(1)} %fusion.43), channel_id=1, source_target_pairs={{0,4},{4,8},{8,12},{12,16},{16,20},{20,24},{24,28},{1,5},{5,9},{9,... | collective-permute-start | bytes 190472 | tf_op jit(solution)/shard_map/ppermute | solution.py:18
  129.2 4.4 %collective-permute-done.3 = f32[2,2,16,4,62]{4,2,3,1,0:T(8,128)S(1)} collective-permute-done((f32[2,2,16,4,62]{4,2,3,1,0:T(8,128)S(1)}, f32[2,2,16,4,62]{4,2,3,1,0:T(8,128)S(1)}, u32[]{:S(2)}, u32[]{:S(2)}) %collective-permute-start.3) | collective-permute-done | bytes 63520 | tf_op jit(solution)/shard_map/ppermute | solution.py:21
  136.5 20.9 %all-reduce = (f32[]{:T(128)}, f32[]{:T(128)}, f32[]{:T(128)}, f32[]{:T(128)}) all-reduce(f32[]{:T(128)S(6)} %mul.1375, f32[]{:T(128)} %get-tuple-element.22, f32[]{:T(128)S(6)} %mul.1372, f32[]{:T(128)} %get-tuple-element.20), channel_id=1, replica_groups=mesh['chan'=8,'slot'=4] {'chan'}, use_global_device_ids=true, to_apply=%region_17.0 | all-reduce | flops 4 | bytes 32 | tf_op jit(solution)/shard_map/psum | solution.py:85
  (55 shorter events, 23.4 us)
Async XLA Ops:
  32.5 4.7 %copy-start = (f32[1,2,16,4,1,3844]{5,2,3,1,4,0:T(8,128)S(1)}, f32[1,2,16,4,1,3844]{5,2,3,1,4,0:T(8,128)}, u32[]{:S(2)}) copy-start(f32[1,2,16,4,1,3844]{5,2,3,1,4,0:T(8,128)} %mul.1258) | copy-start | bytes 5904388
  32.5 4.7 %copy-start.1 = (f32[1,2,16,4,1,3844]{5,2,3,1,4,0:T(8,128)S(1)}, f32[1,2,16,4,1,3844]{5,2,3,1,4,0:T(8,128)}, u32[]{:S(2)}) copy-start(f32[1,2,16,4,1,3844]{5,2,3,1,4,0:T(8,128)} %mul.1262) | copy-start | bytes 5904388
  32.5 4.7 %copy-start.2 = (f32[1,2,16,4,1,3844]{5,2,3,1,4,0:T(8,128)S(1)}, f32[1,2,16,4,1,3844]{5,2,3,1,4,0:T(8,128)}, u32[]{:S(2)}) copy-start(f32[1,2,16,4,1,3844]{5,2,3,1,4,0:T(8,128)} %mul.1265) | copy-start | bytes 5904388
  32.5 4.7 %copy-start.3 = (f32[1,2,16,4,1,3844]{5,2,3,1,4,0:T(8,128)S(1)}, f32[1,2,16,4,1,3844]{5,2,3,1,4,0:T(8,128)}, u32[]{:S(2)}) copy-start(f32[1,2,16,4,1,3844]{5,2,3,1,4,0:T(8,128)} %mul.1270) | copy-start | bytes 5904388
  37.2 2.0 %copy-start.6 = (f32[2,2,4,1,3844]{4,3,2,1,0:T(1,128)S(1)}, f32[2,2,4,1,3844]{4,3,2,1,0:T(1,128)}, u32[]{:S(2)}) copy-start(f32[2,2,4,1,3844]{4,3,2,1,0:T(1,128)} %param.4) | copy-start | bytes 738052
  49.3 9.1 %copy-start.4 = (f32[2,2,16,4,62]{4,3,2,1,0:T(4,128)S(1)}, f32[2,2,16,4,62]{4,3,2,1,0:T(4,128)}, u32[]{:S(2)}) copy-start(f32[2,2,16,4,62]{4,3,2,1,0:T(4,128)} %param.6) | copy-start | bytes 190468
  49.4 9.1 %copy-start.5 = (f32[2,2,16,4,62]{4,3,2,1,0:T(4,128)S(1)}, f32[2,2,16,4,62]{4,3,2,1,0:T(4,128)}, u32[]{:S(2)}) copy-start(f32[2,2,16,4,62]{4,3,2,1,0:T(4,128)} %param.7) | copy-start | bytes 190468
  68.6 52.2 %collective-permute-start = (f32[2,2,16,4,62]{4,2,3,1,0:T(8,128)S(1)}, f32[2,2,16,4,62]{4,2,3,1,0:T(8,128)}, u32[]{:S(2)}, u32[]{:S(2)}) collective-permute-start(f32[2,2,16,4,62]{4,2,3,1,0:T(8,128)S(1)} %copy_add_fusion), channel_id=1, source_target_pairs={{0,4},{4,8},{8,12},{12,16},{16,20},{20,24},{24,28},{1,5},{5,9},{9,... | collective-permute-start | bytes 190472 | tf_op jit(solution)/shard_map/ppermute | solution.py:18
  74.1 46.6 %collective-permute-start.1 = (f32[2,2,16,4,62]{4,2,3,1,0:T(8,128)S(1)}, f32[2,2,16,4,62]{4,2,3,1,0:T(8,128)}, u32[]{:S(2)}, u32[]{:S(2)}) collective-permute-start(f32[2,2,16,4,62]{4,2,3,1,0:T(8,128)S(1)} %copy_add_fusion), channel_id=1, source_target_pairs={{4,0},{8,4},{12,8},{16,12},{20,16},{24,20},{28,24},{5,1},{9,5},{13... | collective-permute-start | bytes 190472 | tf_op jit(solution)/shard_map/ppermute | solution.py:21
  122.1 7.1 %collective-permute-start.2 = (f32[2,2,16,4,62]{4,2,3,1,0:T(8,128)S(1)}, f32[2,2,16,4,62]{4,2,3,1,0:T(8,128)S(1)}, u32[]{:S(2)}, u32[]{:S(2)}) collective-permute-start(f32[2,2,16,4,62]{4,2,3,1,0:T(8,128)S(1)} %fusion.43), channel_id=1, source_target_pairs={{0,4},{4,8},{8,12},{12,16},{16,20},{20,24},{24,28},{1,5},{5,9},{9,... | collective-permute-start | bytes 190472 | tf_op jit(solution)/shard_map/ppermute | solution.py:18
  126.7 6.9 %collective-permute-start.3 = (f32[2,2,16,4,62]{4,2,3,1,0:T(8,128)S(1)}, f32[2,2,16,4,62]{4,2,3,1,0:T(8,128)S(1)}, u32[]{:S(2)}, u32[]{:S(2)}) collective-permute-start(f32[2,2,16,4,62]{4,2,3,1,0:T(8,128)S(1)} %fusion.43), channel_id=1, source_target_pairs={{4,0},{8,4},{12,8},{16,12},{20,16},{24,20},{28,24},{5,1},{9,5},{13... | collective-permute-start | bytes 190472 | tf_op jit(solution)/shard_map/ppermute | solution.py:21
where the time goes:
time: 163 us; the launch traced here: 162 us
  local copies, waits for them, and re-layouts  84.6 us (52%)
  other arithmetic  33.5 us (21%)
  blocking collectives  20.9 us (13%)
  starting transfers between devices  12.7 us (8%)
  waiting for transfers between devices  5.57 us (3%)
  between operations  4.81 us (3%)
    mul x11, local copies, waits for them, and re-layouts, jones_update(): half_real = left_real * sky_real - left_imag * sky_imag  31.1 us
    mul x8, local copies, waits for them, and re-layouts, jones_update(): model_real = half_real * right_real + half_imag * right_imag  28.8 us
    psum x1, blocking collectives, local(): primal, change = lax.psum((pieces[0], pieces[1]), 'chan')  20.9 us
    reduce_sum x2, other arithmetic, jones_update(): jnp.sum(rest_real * weight_real - rest_imag * weight_imag, axis=(3, 5))  19.9 us
    ppermute x2, starting transfers between devices, padded_2(): lax.ppermute(lax.slice_in_dim(block, block.shape[dim] - width, None, axis...  10.1 us
    convert_element_type x1, local copies, waits for them, and re-layouts, jones_update(): sky_real = coherency[0].astype(jnp.float32).reshape(grid_shape)  8.38 us
    convert_element_type x1, local copies, waits for them, and re-layouts, jones_update(): sky_imag = coherency[1].astype(jnp.float32).reshape(grid_shape)  8.23 us
    reduce_sum x2, other arithmetic, jones_update(): jnp.sum(model_imag, axis=1, keepdims=True)  6.56 us
  transfers between devices with their start and end apart: 4, of which 2 were waited for; matrix products, arithmetic and copies ran while one was open for 28% of the time, Pallas kernels for 0%

commit v1 on v0

v1 whole, which is shorter than its diff:
```python
import functools

import jax
import jax.numpy as jnp
from jax import lax
from jax.experimental import pallas as pl
from jax.experimental.pallas import tpu as pltpu
from jax.sharding import PartitionSpec as P

ITERS = 2
HALF = 64
BLOCK = 256
MESH = pl.DeviceIdType.MESH

penalty = 8.0
kernel_taps = (0.04, 0.06, 0.1, 0.15, 0.3, 0.15, 0.1, 0.06, 0.04)


def split(value):
    high = value.astype(jnp.bfloat16)
    return high, (value - high.astype(jnp.float32)).astype(jnp.bfloat16)


def spread_tables(width, blocks, spread_p, spread_q, gather_p):
    def fill(b, carry):
        start = pl.multiple_of(b * BLOCK, BLOCK)
        pair = (lax.broadcasted_iota(jnp.int32, (HALF, BLOCK), 1) + start).astype(jnp.float32)
        station = lax.broadcasted_iota(jnp.int32, (HALF, BLOCK), 0).astype(jnp.float32)
        first = jnp.floor((pair + 0.5) * (1.0 / width))
        second = pair - first * width
        keep = (first != second) & (first < width)
        spread_p[:, pl.ds(start, BLOCK)] = jnp.where((first == station) & keep, 1.0, 0.0).astype(jnp.bfloat16)
        spread_q[:, pl.ds(start, BLOCK)] = jnp.where((second == station) & keep, 1.0, 0.0).astype(jnp.bfloat16)
        pair = (lax.broadcasted_iota(jnp.int32, (BLOCK, 2 * HALF), 0) + start).astype(jnp.float32)
        station = (lax.broadcasted_iota(jnp.int32, (BLOCK, 2 * HALF), 1) & (HALF - 1)).astype(jnp.float32)
        inside = pair - station * width
        keep = (inside >= 0.0) & (inside < width) & (inside != station) & (station < width)
        gather_p[pl.ds(start, BLOCK), :] = jnp.where(keep, 1.0, 0.0).astype(jnp.bfloat16)
        return carry

    lax.fori_loop(0, blocks, fill, 0)


def kernel(
    count, dims,
    vis_in, sky_in, jones_in, duals_in,
    jones_out, consensus_out, duals_out, norms_out,
    vis, sky, spread_p, spread_q, gather_p, lhs, left, right, parts,
    gain, cons, dual, total, summed, from_low, from_high, sums, slots,
    send_sem, low_sem, high_sem, norm_send, norm_recv,
):
    pols, dirs, channels, width, pairs, blocks, entries = dims
    me = lax.axis_index("chan")
    rows = pols * channels
    tall = dirs * rows

    for it in range(ITERS):
        from_low[it] = jnp.zeros_like(from_low[it])
        from_high[it] = jnp.zeros_like(from_high[it])
    barrier = pltpu.get_barrier_semaphore()
    for step in range(1, count):
        pl.semaphore_signal(barrier, inc=1, device_id={"chan": lax.rem(me + step, count)}, device_id_type=MESH)

    spread_tables(width, blocks, spread_p, spread_q, gather_p)
    for part in range(2):
        vis[part] = jnp.zeros_like(vis[part])
        for pol in range(pols):
            for chan in range(channels):
                row = pol * channels + chan
                vis[part, row : row + 1, 0:pairs] = vis_in[part, pol, chan]
    tail = pairs // 128 * 128
    edge = blocks * BLOCK - tail
    sky[:, :, :, pl.ds(tail, edge)] = jnp.zeros((2, dirs, rows, edge), jnp.float32)

    def unpack(k, carry):
        for part in range(2):
            for pol in range(pols):
                sky[part, k, pol * channels : (pol + 1) * channels, 0:pairs] = sky_in[part, pol, k].astype(jnp.float32)
        return carry

    lax.fori_loop(0, dirs, unpack, 0)

    gain[...] = jnp.zeros_like(gain)
    dual[...] = jnp.zeros_like(dual)
    for part in range(2):
        for pol in range(pols):
            at = (slice(None), slice(pol * channels, (pol + 1) * channels), slice(part * HALF, part * HALF + width))
            gain[at] = jones_in[part, pol]
            dual[at] = duals_in[part, pol]
    cons[...] = gain[...]
    sums[...] = jnp.zeros_like(sums)

    row = lax.broadcasted_iota(jnp.int32, (rows, 128), 0) % channels

    def taps(distance, shift, low, high):
        offset = distance + shift + 4
        if offset < 0 or offset > 8:
            return None
        inside = (row + shift >= low) & (row + shift < high)
        return jnp.where(inside, kernel_taps[offset], 0.0)

    def mixed(block, distance):
        out = None
        for shift in range(1 - channels, channels):
            weight = taps(distance, shift, 0, channels)
            if weight is None:
                continue
            moved = block if shift == 0 else pltpu.roll(block, (-shift) % rows, 1)
            term = weight[None] * moved
            out = term if out is None else out + term
        return out

    def norm_copy(step):
        return pltpu.make_async_remote_copy(
            src_ref=sums, dst_ref=slots.at[me],
            send_sem=norm_send.at[step], recv_sem=norm_recv.at[step],
            device_id={"chan": lax.rem(me + step, count)}, device_id_type=MESH,
        )

    for it in range(ITERS):
        now = gain[...].reshape(tall, 128)
        high, low = split(now)
        lhs[0:tall, 0:128] = high
        lhs[0:tall, 128:256] = low
        high, low = split(pltpu.roll(now, HALF, 1))
        lhs[tall:, 0:128] = high
        lhs[tall:, 128:256] = low
        total[...] = jnp.zeros_like(total)

        def block_step(b, carry):
            start = pl.multiple_of(b * BLOCK, BLOCK)
            zeros = jnp.zeros((HALF, BLOCK), jnp.bfloat16)
            ep = spread_p[:, pl.ds(start, BLOCK)]
            eq = spread_q[:, pl.ds(start, BLOCK)]
            left[...] = jnp.dot(lhs[...], jnp.concatenate([ep, zeros, ep, zeros], 0), preferred_element_type=jnp.float32)
            right[...] = jnp.dot(lhs[...], jnp.concatenate([eq, zeros, eq, zeros], 0), preferred_element_type=jnp.float32)
            for lane in range(0, BLOCK, 128):
                lanes = pl.ds(pl.multiple_of(start + lane, 128), 128)
                model_r = jnp.zeros((rows, 128), jnp.float32)
                model_i = jnp.zeros((rows, 128), jnp.float32)
                held = []
                for k in range(dirs):
                    sr, si = sky[0, k, :, lanes], sky[1, k, :, lanes]
                    mine = slice(k * rows, (k + 1) * rows)
                    other = slice(tall + k * rows, tall + (k + 1) * rows)
                    here = slice(lane, lane + 128)
                    rr, ri = right[mine, here], right[other, here]
                    lr, li = left[mine, here], left[other, here]
                    zr = sr * rr + si * ri
                    zi = sr * ri - si * rr
                    model_r = model_r + (lr * zr + li * zi)
                    model_i = model_i + (li * zr - lr * zi)
                    held.append((zr, zi))
                dr = vis[0, :, lanes] - model_r
                di = vis[1, :, lanes] - model_i
                for k in range(0, dirs, 2):
                    pair = held[k : k + 2]
                    values = (
                        [dr * zr - di * zi for zr, zi in pair],
                        [dr * zi + di * zr for zr, zi in pair],
                        [zr * zr + zi * zi for zr, zi in pair],
                    )
                    for i, value in enumerate(values):
                        high, low = split(jnp.concatenate(value, 0))
                        at = slice(i * tall + k * rows, i * tall + (k + 2) * rows)
                        parts[0, at, lane : lane + 128] = high
                        parts[1, at, lane : lane + 128] = low
            weight = gather_p[pl.ds(start, BLOCK), :]
            total[...] += jnp.dot(parts[0], weight, preferred_element_type=jnp.float32) + jnp.dot(
                parts[1], weight, preferred_element_type=jnp.float32
            )
            return carry

        lax.fori_loop(0, blocks, block_step, 0)

        lane = lax.broadcasted_iota(jnp.int32, (tall, 128), 1)
        upper = jnp.where(lane < HALF, total[0:tall], total[tall : 2 * tall]).reshape(dirs, rows, 128)
        lower = total[2 * tall :].reshape(dirs, rows, 128)
        fresh_gain = (upper + gain[...] * lower + penalty * (cons[...] - dual[...])) / (lower + penalty)
        gain[...] = fresh_gain
        summed[it] = fresh_gain + dual[...]

        def halo(direction):
            return pltpu.make_async_remote_copy(
                src_ref=summed.at[it],
                dst_ref=(from_low if direction > 0 else from_high).at[it],
                send_sem=send_sem.at[it, 0 if direction > 0 else 1],
                recv_sem=(low_sem if direction > 0 else high_sem).at[it],
                device_id={"chan": lax.rem(me + direction + count, count)}, device_id_type=MESH,
            )

        if it == 0:
            pl.semaphore_wait(barrier, count - 1)
        up, down = halo(1), halo(-1)

        @pl.when(me < count - 1)
        def _():
            up.start()

        @pl.when(me > 0)
        def _():
            down.start()

        own = mixed(summed[it], 0)

        @pl.when(me > 0)
        def _():
            up.wait_recv()

        @pl.when(me < count - 1)
        def _():
            down.wait_recv()

        fresh = own + mixed(from_low[it], -channels) + mixed(from_high[it], channels)
        gap = gain[...] - fresh
        moved = fresh - cons[...]
        dual[...] = dual[...] + gap
        cons[...] = fresh
        primal = jnp.sum(jnp.sum(gap * gap, 0), 0, keepdims=True)
        change = jnp.sum(jnp.sum(moved * moved, 0), 0, keepdims=True)
        sums[2 * it : 2 * it + 1] = primal
        sums[2 * it + 1 : 2 * it + 2] = change

    slots[pl.ds(me, 1)] = sums[...][None]
    for step in range(1, count):
        norm_copy(step).start()

    for part in range(2):
        for pol in range(pols):
            at = (slice(None), slice(pol * channels, (pol + 1) * channels), slice(part * HALF, part * HALF + width))
            jones_out[part, pol] = gain[at]
            consensus_out[part, pol] = cons[at]
            duals_out[part, pol] = dual[at]

    for it in range(ITERS):

        @pl.when(me < count - 1)
        def _():
            pltpu.make_async_remote_copy(
                src_ref=summed.at[it], dst_ref=from_low.at[it], send_sem=send_sem.at[it, 0], recv_sem=low_sem.at[it],
                device_id={"chan": lax.rem(me + 1, count)}, device_id_type=MESH,
            ).wait_send()

        @pl.when(me > 0)
        def _():
            pltpu.make_async_remote_copy(
                src_ref=summed.at[it], dst_ref=from_high.at[it], send_sem=send_sem.at[it, 1], recv_sem=high_sem.at[it],
                device_id={"chan": lax.rem(me - 1 + count, count)}, device_id_type=MESH,
            ).wait_send()

    for step in range(1, count):
        norm_copy(step).wait()
    gathered = slots[0]
    for j in range(1, count):
        gathered = gathered + slots[j]
    folded = jnp.sum(gathered, axis=1, keepdims=True) * (1.0 / entries)
    for it in range(ITERS):
        norms_out[it : it + 1, 0:1] = folded[2 * it : 2 * it + 1]
        norms_out[it : it + 1, 1:2] = folded[2 * it + 1 : 2 * it + 2] * (penalty * penalty)


def solution(mesh):
    count = mesh.shape["chan"]

    def local(visibility, coherency, jones_start, duals_start):
        _, pols, dirs, channels, width = jones_start.shape
        pairs = visibility.shape[-1]
        times = visibility.shape[3]
        assert times == 1 and channels == 4 and pols * channels == 8 and width <= HALF - 2
        blocks = pl.cdiv(pairs, BLOCK)
        long = blocks * BLOCK
        rows, tall = pols * channels, dirs * pols * channels
        entries = jones_start.size * count
        sky = coherency.transpose(0, 1, 2, 4, 3, 5).reshape(2, pols, dirs, channels, pairs)
        state = jax.ShapeDtypeStruct(jones_start.shape, jnp.float32)
        f32, bf16 = jnp.float32, jnp.bfloat16
        packed = (dirs, rows, 2 * HALF)
        return pl.pallas_call(
            functools.partial(kernel, count, (pols, dirs, channels, width, pairs, blocks, entries)),
            out_shape=(state, state, state, jax.ShapeDtypeStruct((ITERS, 2), f32)),
            in_specs=[pl.BlockSpec(memory_space=pltpu.VMEM)] * 4,
            out_specs=tuple([pl.BlockSpec(memory_space=pltpu.VMEM)] * 4),
            scratch_shapes=[
                pltpu.VMEM((2, rows, long), f32),
                pltpu.VMEM((2, dirs, rows, long), f32),
                pltpu.VMEM((HALF, long), bf16),
                pltpu.VMEM((HALF, long), bf16),
                pltpu.VMEM((long, 2 * HALF), bf16),
                pltpu.VMEM((2 * tall, 4 * HALF), bf16),
                pltpu.VMEM((2 * tall, BLOCK), f32),
                pltpu.VMEM((2 * tall, BLOCK), f32),
                pltpu.VMEM((2, 3 * tall, BLOCK), bf16),
                pltpu.VMEM(packed, f32),
                pltpu.VMEM(packed, f32),
                pltpu.VMEM(packed, f32),
                pltpu.VMEM((3 * tall, 2 * HALF), f32),
                pltpu.VMEM((ITERS,) + packed, f32),
                pltpu.VMEM((ITERS,) + packed, f32),
                pltpu.VMEM((ITERS,) + packed, f32),
                pltpu.VMEM((8, 2 * HALF), f32),
                pltpu.VMEM((count, 8, 2 * HALF), f32),
                pltpu.SemaphoreType.DMA((ITERS, 2)),
                pltpu.SemaphoreType.DMA((ITERS,)),
                pltpu.SemaphoreType.DMA((ITERS,)),
                pltpu.SemaphoreType.DMA((count,)),
                pltpu.SemaphoreType.DMA((count,)),
            ],
            compiler_params=pltpu.CompilerParams(
                collective_id=0, has_side_effects=True, vmem_limit_bytes=48 * 1024 * 1024
            ),
        )(visibility, sky, jones_start, duals_start)

    placed = (
        P(None, None, "chan", "slot", None),
        P(None, None, None, "chan", "slot", None),
        P(None, None, "slot", "chan", None),
        P(None, None, "slot", "chan", None),
    )
    return jax.shard_map(
        local,
        mesh=mesh,
        in_specs=placed,
        out_specs=(
            P(None, None, "slot", "chan", None),
            P(None, None, "slot", "chan", None),
            P(None, None, "slot", "chan", None),
            P("slot", None),
        ),
        check_vma=False,
    )
```

time: 163 us -> 43 us (0.26)
  local copies, waits for them, and re-layouts: 84.6 us -> 6.84 us
  Pallas kernels: 0 us -> 35.3 us
  other arithmetic: 33.5 us -> 0 us
  blocking collectives: 20.9 us -> 0 us
  starting transfers between devices: 12.7 us -> 0 us
  waiting for transfers between devices: 5.57 us -> 0 us
  between operations: 4.81 us -> 0.65 us
    mul x19 -> x0, local copies, waits for them, and re-layouts: 59.9 us -> none  [the longest x11 31.1 us: jones_update(): half_real = left_real * sky_real - left_imag * sky_imag]
    pallas_call x0 -> x1, Pallas kernels: none -> 35.3 us  [local(): pl.pallas_call(functools.partial(kernel, count, (pols, dirs, channels, wi...]
    reduce_sum x5 -> x0, other arithmetic: 27.4 us -> none  [the longest x2 19.9 us: jones_update(): jnp.sum(rest_real * weight_real - rest_imag * weight_imag, axis=(3, 5))]
    psum x1 -> x0, blocking collectives: 20.9 us -> none  [local(): primal, change = lax.psum((pieces[0], pieces[1]), 'chan')]
    convert_element_type x2 -> x0, local copies, waits for them, and re-layouts: 16.6 us -> none  [the longest x1 8.38 us: jones_update(): sky_real = coherency[0].astype(jnp.float32).reshape(grid_shape)]
    ppermute x4 -> x0, starting transfers between devices: 12.7 us -> none  [the longest x2 10.1 us: padded_2(): lax.ppermute(lax.slice_in_dim(block, block.shape[dim] - width, None, axis...]
    ppermute x4 -> x0, waiting for transfers between devices: 5.57 us -> none  [the longest x2 4.37 us: padded_2(): lax.ppermute(lax.slice_in_dim(block, 0, width, axis=dim), axis, backward)]
    unnamed x17 -> x12, local copies, waits for them, and re-layouts: 2.15 us -> 6.84 us
  transfers between devices with their start and end apart: 4 -> 0, of which waited for: 2 -> 0; matrix products, arithmetic and copies ran while one was open for 28% -> 0% of each run, Pallas kernels for 0% -> 0%
where the time goes in v1:
time: 43 us; the launch traced here: 42.8 us
  Pallas kernels  35.3 us (82%)
  local copies, waits for them, and re-layouts  6.84 us (16%)
  between operations  0.65 us (2%)
    pallas_call x1, Pallas kernels, local(): pl.pallas_call(functools.partial(kernel, count, (pols, dirs, channels, wi...  35.3 us
    unnamed x12, local copies, waits for them, and re-layouts  6.84 us

profile of v1, /device:TPU:0, one launch (start us, length us, event | category | flops | bytes accessed | tf_op | source)
XLA Modules:
  0.0 42.8 jit_solution(6697041669290756095)
XLA Ops:
  0.6 0.0 copy-start
  0.6 1.6 %copy-done = bf16[2,2,16,4,1,3844]{5,3,4,2,1,0:T(4,128)(2,1)S(1)} copy-done((bf16[2,2,16,4,1,3844]{5,3,4,2,1,0:T(4,128)(2,1)S(1)}, bf16[2,2,16,4,1,3844]{5,3,4,2,1,0:T(4,128)(2,1)}, u32[]{:S(2)}) %copy-start) | copy-done | bytes 1968152
  2.2 0.0 copy-start.1
  2.2 0.9 %copy-done.1 = f32[2,2,4,1,3844]{4,3,2,1,0:T(1,128)S(1)} copy-done((f32[2,2,4,1,3844]{4,3,2,1,0:T(1,128)S(1)}, f32[2,2,4,1,3844]{4,3,2,1,0:T(1,128)}, u32[]{:S(2)}) %copy-start.1) | copy-done | bytes 246040
  3.1 0.0 copy-start.2
  3.2 0.9 %copy-done.2 = f32[2,2,16,4,62]{4,3,2,1,0:T(4,128)S(1)} copy-done((f32[2,2,16,4,62]{4,3,2,1,0:T(4,128)S(1)}, f32[2,2,16,4,62]{4,3,2,1,0:T(4,128)}, u32[]{:S(2)}) %copy-start.2) | copy-done | bytes 63512
  4.1 0.0 copy-start.3
  4.1 0.9 %copy-done.3 = f32[2,2,16,4,62]{4,3,2,1,0:T(4,128)S(1)} copy-done((f32[2,2,16,4,62]{4,3,2,1,0:T(4,128)S(1)}, f32[2,2,16,4,62]{4,3,2,1,0:T(4,128)}, u32[]{:S(2)}) %copy-start.3) | copy-done | bytes 63512
  5.0 35.3 %shard_map.75 = (f32[2,2,16,4,62]{4,3,2,1,0:T(4,128)S(1)}, f32[2,2,16,4,62]{4,3,2,1,0:T(4,128)S(1)}, f32[2,2,16,4,62]{4,3,2,1,0:T(4,128)S(1)}, f32[2,2]{1,0:T(2,128)S(1)}) custom-call(f32[2,2,4,1,3844]{4,3,2,1,0:T(1,128)S(1)} %copy-done.1, bf16[2,2,16,4,3844]{4,3,2,1,0:T(4,128)(2,1)S(1)} %bitcast.1, f32[2,2,16,4,62]{4,3,2,1,0:T(4,128)S(1)} %copy-done.2, ...), custom_call_target="tpu_custom_call" | custom-call | tf_op jit(solution)/shard_map/pallas_call | solution.py:278
  40.2 0.7 %copy.12 = f32[2,2,16,4,62]{4,3,2,1,0:T(4,128)} copy(f32[2,2,16,4,62]{4,3,2,1,0:T(4,128)S(1)} %get-tuple-element.8) | data formatting | bytes 126976
  40.9 0.7 %copy.13 = f32[2,2,16,4,62]{4,3,2,1,0:T(4,128)} copy(f32[2,2,16,4,62]{4,3,2,1,0:T(4,128)S(1)} %get-tuple-element.9) | data formatting | bytes 126976
  41.6 0.7 %copy.14 = f32[2,2,16,4,62]{4,3,2,1,0:T(4,128)} copy(f32[2,2,16,4,62]{4,3,2,1,0:T(4,128)S(1)} %get-tuple-element.10) | data formatting | bytes 126976
  42.2 0.6 %copy.15 = f32[2,2]{1,0:T(2,128)} copy(f32[2,2]{1,0:T(2,128)S(1)} %get-tuple-element.11) | data formatting | bytes 32
Async XLA Ops:
  0.6 1.6 %copy-start = (bf16[2,2,16,4,1,3844]{5,3,4,2,1,0:T(4,128)(2,1)S(1)}, bf16[2,2,16,4,1,3844]{5,3,4,2,1,0:T(4,128)(2,1)}, u32[]{:S(2)}) copy-start(bf16[2,2,16,4,1,3844]{5,3,4,2,1,0:T(4,128)(2,1)} %param.5) | copy-start | bytes 5904388
  2.2 0.9 %copy-start.1 = (f32[2,2,4,1,3844]{4,3,2,1,0:T(1,128)S(1)}, f32[2,2,4,1,3844]{4,3,2,1,0:T(1,128)}, u32[]{:S(2)}) copy-start(f32[2,2,4,1,3844]{4,3,2,1,0:T(1,128)} %vis_in.1) | copy-start | bytes 738052
  3.1 0.9 %copy-start.2 = (f32[2,2,16,4,62]{4,3,2,1,0:T(4,128)S(1)}, f32[2,2,16,4,62]{4,3,2,1,0:T(4,128)}, u32[]{:S(2)}) copy-start(f32[2,2,16,4,62]{4,3,2,1,0:T(4,128)} %jones_in.1) | copy-start | bytes 190468
  4.1 0.9 %copy-start.3 = (f32[2,2,16,4,62]{4,3,2,1,0:T(4,128)S(1)}, f32[2,2,16,4,62]{4,3,2,1,0:T(4,128)}, u32[]{:S(2)}) copy-start(f32[2,2,16,4,62]{4,3,2,1,0:T(4,128)} %duals_in.1) | copy-start | bytes 190468

commit v2 on v1

v2 whole, which is shorter than its diff:
```python
import functools

import jax
import jax.numpy as jnp
from jax import lax
from jax.experimental import pallas as pl
from jax.experimental.pallas import tpu as pltpu
from jax.sharding import PartitionSpec as P

ITERS = 2
HALF = 64
BLOCK = 256
UNROLL = 2
MESH = pl.DeviceIdType.MESH

penalty = 8.0
kernel_taps = (0.04, 0.06, 0.1, 0.15, 0.3, 0.15, 0.1, 0.06, 0.04)


def split(value):
    high = value.astype(jnp.bfloat16)
    return high, (value - high.astype(jnp.float32)).astype(jnp.bfloat16)


def spread_tables(width, blocks, spread_p, spread_q, gather_p):
    def fill(b, carry):
        start = pl.multiple_of(b * BLOCK, BLOCK)
        pair = (lax.broadcasted_iota(jnp.int32, (HALF, BLOCK), 1) + start).astype(jnp.float32)
        station = lax.broadcasted_iota(jnp.int32, (HALF, BLOCK), 0).astype(jnp.float32)
        first = jnp.floor((pair + 0.5) * (1.0 / width))
        second = pair - first * width
        keep = (first != second) & (first < width)
        spread_p[:, pl.ds(start, BLOCK)] = jnp.where((first == station) & keep, 1.0, 0.0).astype(jnp.bfloat16)
        spread_q[:, pl.ds(start, BLOCK)] = jnp.where((second == station) & keep, 1.0, 0.0).astype(jnp.bfloat16)
        pair = (lax.broadcasted_iota(jnp.int32, (BLOCK, 2 * HALF), 0) + start).astype(jnp.float32)
        station = (lax.broadcasted_iota(jnp.int32, (BLOCK, 2 * HALF), 1) & (HALF - 1)).astype(jnp.float32)
        inside = pair - station * width
        keep = (inside >= 0.0) & (inside < width) & (inside != station) & (station < width)
        gather_p[pl.ds(start, BLOCK), :] = jnp.where(keep, 1.0, 0.0).astype(jnp.bfloat16)
        return carry

    lax.fori_loop(0, blocks, fill, 0)


def kernel(
    count, dims,
    vis_in, sky_in, jones_in, duals_in,
    jones_out, consensus_out, duals_out, norms_out,
    vis_raw, sky_raw, jones_raw, duals_raw,
    vis, sky, spread_p, spread_q, gather_p, lhs, left, right, parts,
    gain, cons, dual, total, summed, from_low, from_high, sums, slots,
    load_sem, sky_sem, send_sem, low_sem, high_sem, norm_send, norm_recv,
):
    pols, dirs, channels, width, pairs, blocks, entries = dims
    me = lax.axis_index("chan")
    group = 8 // channels
    tiles = dirs // group
    tall = tiles * 8

    loads = [
        pltpu.make_async_copy(source, target, load_sem.at[i])
        for i, (source, target) in enumerate(((vis_in, vis_raw), (jones_in, jones_raw), (duals_in, duals_raw)))
    ]
    sky_loads = [
        [pltpu.make_async_copy(sky_in.at[part, pol], sky_raw.at[part, pol], sky_sem.at[part, pol]) for part in range(2)]
        for pol in range(pols)
    ]
    for copy in loads + [copy for per_pol in sky_loads for copy in per_pol]:
        copy.start()

    from_low[...] = jnp.zeros_like(from_low)
    from_high[...] = jnp.zeros_like(from_high)
    barrier = pltpu.get_barrier_semaphore()
    for step in range(1, count):
        pl.semaphore_signal(barrier, inc=1, device_id={"chan": lax.rem(me + step, count)}, device_id_type=MESH)

    spread_tables(width, blocks, spread_p, spread_q, gather_p)
    tail = pairs // 128 * 128
    edge = blocks * BLOCK - tail
    vis[:, :, :, pl.ds(tail, edge)] = jnp.zeros((2, pols, 8, edge), jnp.float32)
    sky[:, :, :, :, pl.ds(tail, edge)] = jnp.zeros((2, pols, tiles, 8, edge), jnp.float32)
    gain[...] = jnp.zeros_like(gain)
    dual[...] = jnp.zeros_like(dual)
    sums[...] = jnp.zeros_like(sums)
    for copy in loads:
        copy.wait()
    for part in range(2):
        for pol in range(pols):
            for row in range(8):
                vis[part, pol, row : row + 1, 0:pairs] = vis_raw[part, pol, row % channels]
            for lead in range(group):
                rows = slice(lead * channels, (lead + 1) * channels)
                lanes = slice(part * HALF, part * HALF + width)
                for tile in range(tiles):
                    gain[pol, tile, rows, lanes] = jones_raw[part, pol, tile * group + lead]
                    dual[pol, tile, rows, lanes] = duals_raw[part, pol, tile * group + lead]
    cons[...] = gain[...]

    def unpack(pol):
        for copy in sky_loads[pol]:
            copy.wait()

        def one(tile, carry):
            for part in range(2):
                for lead in range(group):
                    rows = slice(lead * channels, (lead + 1) * channels)
                    sky[part, pol, tile, rows, 0:pairs] = sky_raw[part, pol, tile * group + lead].astype(jnp.float32)
            return carry

        lax.fori_loop(0, tiles, one, 0)

    def solve(pol):
        now = gain[pol].reshape(tall, 128)
        high, low = split(now)
        lhs[pol, 0:tall, 0:128] = high
        lhs[pol, 0:tall, 128:256] = low
        high, low = split(pltpu.roll(now, HALF, 1))
        lhs[pol, tall:, 0:128] = high
        lhs[pol, tall:, 128:256] = low
        total[...] = jnp.zeros_like(total)

        def one_block(start, u):
            zeros = jnp.zeros((HALF, BLOCK), jnp.bfloat16)
            ep = spread_p[:, pl.ds(start, BLOCK)]
            eq = spread_q[:, pl.ds(start, BLOCK)]
            gains = lhs[pol]
            left[u] = jnp.dot(gains, jnp.concatenate([ep, zeros, ep, zeros], 0), preferred_element_type=jnp.float32)
            right[u] = jnp.dot(gains, jnp.concatenate([eq, zeros, eq, zeros], 0), preferred_element_type=jnp.float32)
            for lane in range(0, BLOCK, 128):
                lanes = pl.ds(pl.multiple_of(start + lane, 128), 128)
                here = slice(lane, lane + 128)
                model_r = jnp.zeros((8, 128), jnp.float32)
                model_i = jnp.zeros((8, 128), jnp.float32)
                held = []
                for t in range(tiles):
                    sr, si = sky[0, pol, t, :, lanes], sky[1, pol, t, :, lanes]
                    mine = slice(t * 8, (t + 1) * 8)
                    other = slice(tall + t * 8, tall + (t + 1) * 8)
                    rr, ri = right[u, mine, here], right[u, other, here]
                    lr, li = left[u, mine, here], left[u, other, here]
                    zr = sr * rr + si * ri
                    zi = sr * ri - si * rr
                    model_r = model_r + (lr * zr + li * zi)
                    model_i = model_i + (li * zr - lr * zi)
                    held.append((zr, zi))
                all_r, all_i = model_r, model_i
                for lead in range(1, group):
                    all_r = all_r + pltpu.roll(model_r, lead * channels, 0)
                    all_i = all_i + pltpu.roll(model_i, lead * channels, 0)
                dr = vis[0, pol, :, lanes] - all_r
                di = vis[1, pol, :, lanes] - all_i
                for t in range(0, tiles, 2):
                    pair = held[t : t + 2]
                    values = (
                        [dr * zr - di * zi for zr, zi in pair],
                        [dr * zi + di * zr for zr, zi in pair],
                        [zr * zr + zi * zi for zr, zi in pair],
                    )
                    for i, value in enumerate(values):
                        high, low = split(jnp.concatenate(value, 0))
                        at = slice(i * tall + t * 8, i * tall + (t + 2) * 8)
                        parts[u, 0, at, here] = high
                        parts[u, 1, at, here] = low
            weight = gather_p[pl.ds(start, BLOCK), :]
            return jnp.dot(parts[u, 0], weight, preferred_element_type=jnp.float32) + jnp.dot(
                parts[u, 1], weight, preferred_element_type=jnp.float32
            )

        def several(b, carry):
            added = None
            for u in range(UNROLL):
                start = pl.multiple_of((b * UNROLL + u) * BLOCK, BLOCK)
                term = one_block(start, u)
                added = term if added is None else added + term
            total[...] += added
            return carry

        lax.fori_loop(0, blocks // UNROLL, several, 0)

        lane = lax.broadcasted_iota(jnp.int32, (tall, 128), 1)
        upper = jnp.where(lane < HALF, total[0:tall], total[tall : 2 * tall]).reshape(tiles, 8, 128)
        lower = total[2 * tall :].reshape(tiles, 8, 128)
        fresh = (upper + gain[pol] * lower + penalty * (cons[pol] - dual[pol])) / (lower + penalty)
        gain[pol] = fresh
        return fresh

    row = lax.broadcasted_iota(jnp.int32, (8, 128), 0) % channels

    def mixed(block, distance):
        out = None
        for shift in range(1 - channels, channels):
            offset = distance + shift + 4
            if offset < 0 or offset > 8:
                continue
            inside = (row + shift >= 0) & (row + shift < channels)
            weight = jnp.where(inside, kernel_taps[offset], 0.0)
            moved = block if shift == 0 else pltpu.roll(block, (-shift) % 8, 1)
            term = weight[None] * moved
            out = term if out is None else out + term
        return out

    def up_copy(it, pol):
        return pltpu.make_async_remote_copy(
            src_ref=summed.at[it, pol], dst_ref=from_low.at[it, pol],
            send_sem=send_sem.at[it, pol, 0], recv_sem=low_sem.at[it, pol],
            device_id={"chan": lax.rem(me + 1, count)}, device_id_type=MESH,
        )

    def down_copy(it, pol):
        return pltpu.make_async_remote_copy(
            src_ref=summed.at[it, pol], dst_ref=from_high.at[it, pol],
            send_sem=send_sem.at[it, pol, 1], recv_sem=high_sem.at[it, pol],
            device_id={"chan": lax.rem(me + count - 1, count)}, device_id_type=MESH,
        )

    def send(it, pol, fresh):
        summed[it, pol] = fresh + dual[pol]

        @pl.when(me < count - 1)
        def _():
            up_copy(it, pol).start()

        @pl.when(me > 0)
        def _():
            down_copy(it, pol).start()

    def smooth(it, pol):
        own = mixed(summed[it, pol], 0)

        @pl.when(me > 0)
        def _():
            up_copy(it, pol).wait_recv()

        @pl.when(me < count - 1)
        def _():
            down_copy(it, pol).wait_recv()

        fresh = own + mixed(from_low[it, pol], -channels) + mixed(from_high[it, pol], channels)
        gap = gain[pol] - fresh
        moved = fresh - cons[pol]
        dual[pol] = dual[pol] + gap
        cons[pol] = fresh
        sums[2 * it : 2 * it + 1] += jnp.sum(jnp.sum(gap * gap, 0), 0, keepdims=True)
        sums[2 * it + 1 : 2 * it + 2] += jnp.sum(jnp.sum(moved * moved, 0), 0, keepdims=True)

    def norm_copy(step):
        return pltpu.make_async_remote_copy(
            src_ref=sums, dst_ref=slots.at[me],
            send_sem=norm_send.at[step], recv_sem=norm_recv.at[step],
            device_id={"chan": lax.rem(me + step, count)}, device_id_type=MESH,
        )

    def put(target, state, pol):
        for part in range(2):
            lanes = slice(part * HALF, part * HALF + width)
            for lead in range(group):
                rows = slice(lead * channels, (lead + 1) * channels)
                for tile in range(tiles):
                    target[part, pol, tile * group + lead] = state[pol, tile, rows, lanes]

    for it in range(ITERS):
        for pol in range(pols):
            if it == 0:
                unpack(pol)
            else:
                smooth(it - 1, pol)
            fresh = solve(pol)
            if it == 0 and pol == 0:
                pl.semaphore_wait(barrier, count - 1)
            send(it, pol, fresh)
    for pol in range(pols):
        put(jones_out, gain, pol)
    for pol in range(pols):
        smooth(ITERS - 1, pol)

    slots[pl.ds(me, 1)] = sums[...][None]
    for step in range(1, count):
        norm_copy(step).start()
    for pol in range(pols):
        put(consensus_out, cons, pol)
        put(duals_out, dual, pol)

    for it in range(ITERS):
        for pol in range(pols):

            @pl.when(me < count - 1)
            def _():
                up_copy(it, pol).wait_send()

            @pl.when(me > 0)
            def _():
                down_copy(it, pol).wait_send()

    for step in range(1, count):
        norm_copy(step).wait()
    gathered = slots[0]
    for j in range(1, count):
        gathered = gathered + slots[j]
    folded = jnp.sum(gathered, axis=1, keepdims=True) * (1.0 / entries)
    for it in range(ITERS):
        norms_out[it : it + 1, 0:1] = folded[2 * it : 2 * it + 1]
        norms_out[it : it + 1, 1:2] = folded[2 * it + 1 : 2 * it + 2] * (penalty * penalty)


def solution(mesh):
    count = mesh.shape["chan"]

    def local(visibility, coherency, jones_start, duals_start):
        _, pols, dirs, channels, width = jones_start.shape
        pairs = visibility.shape[-1]
        times = visibility.shape[3]
        assert times == 1 and channels == 4 and dirs % 4 == 0 and width <= HALF - 2
        blocks = pl.cdiv(pairs, BLOCK * UNROLL) * UNROLL
        long = blocks * BLOCK
        tiles = dirs * channels // 8
        tall = tiles * 8
        entries = jones_start.size * count
        sky = coherency.transpose(0, 1, 2, 4, 3, 5).reshape(2, pols, dirs, channels, pairs)
        state = jax.ShapeDtypeStruct(jones_start.shape, jnp.float32)
        f32, bf16 = jnp.float32, jnp.bfloat16
        packed = (pols, tiles, 8, 2 * HALF)
        return pl.pallas_call(
            functools.partial(kernel, count, (pols, dirs, channels, width, pairs, blocks, entries)),
            out_shape=(state, state, state, jax.ShapeDtypeStruct((ITERS, 2), f32)),
            in_specs=[pl.BlockSpec(memory_space=pl.ANY)] * 4,
            out_specs=tuple([pl.BlockSpec(memory_space=pltpu.VMEM)] * 4),
            scratch_shapes=[
                pltpu.VMEM(visibility.shape, f32),
                pltpu.VMEM(sky.shape, bf16),
                pltpu.VMEM(jones_start.shape, f32),
                pltpu.VMEM(duals_start.shape, f32),
                pltpu.VMEM((2, pols, 8, long), f32),
                pltpu.VMEM((2, pols, tiles, 8, long), f32),
                pltpu.VMEM((HALF, long), bf16),
                pltpu.VMEM((HALF, long), bf16),
                pltpu.VMEM((long, 2 * HALF), bf16),
                pltpu.VMEM((pols, 2 * tall, 4 * HALF), bf16),
                pltpu.VMEM((UNROLL, 2 * tall, BLOCK), f32),
                pltpu.VMEM((UNROLL, 2 * tall, BLOCK), f32),
                pltpu.VMEM((UNROLL, 2, 3 * tall, BLOCK), bf16),
                pltpu.VMEM(packed, f32),
                pltpu.VMEM(packed, f32),
                pltpu.VMEM(packed, f32),
                pltpu.VMEM((3 * tall, 2 * HALF), f32),
                pltpu.VMEM((ITERS,) + packed, f32),
                pltpu.VMEM((ITERS,) + packed, f32),
                pltpu.VMEM((ITERS,) + packed, f32),
                pltpu.VMEM((8, 2 * HALF), f32),
                pltpu.VMEM((count, 8, 2 * HALF), f32),
                pltpu.SemaphoreType.DMA((3,)),
                pltpu.SemaphoreType.DMA((2, pols)),
                pltpu.SemaphoreType.DMA((ITERS, pols, 2)),
                pltpu.SemaphoreType.DMA((ITERS, pols)),
                pltpu.SemaphoreType.DMA((ITERS, pols)),
                pltpu.SemaphoreType.DMA((count,)),
                pltpu.SemaphoreType.DMA((count,)),
            ],
            compiler_params=pltpu.CompilerParams(
                collective_id=0, has_side_effects=True, vmem_limit_bytes=60 * 1024 * 1024
            ),
        )(visibility, sky, jones_start, duals_start)

    placed = (
        P(None, None, "chan", "slot", None),
        P(None, None, None, "chan", "slot", None),
        P(None, None, "slot", "chan", None),
        P(None, None, "slot", "chan", None),
    )
    return jax.shard_map(
        local,
        mesh=mesh,
        in_specs=placed,
        out_specs=(
            P(None, None, "slot", "chan", None),
            P(None, None, "slot", "chan", None),
            P(None, None, "slot", "chan", None),
            P("slot", None),
        ),
        check_vma=False,
    )
```

time: 43 us -> 42 us (0.977)
  local copies, waits for them, and re-layouts: 6.84 us -> 5.9 us
    unnamed x12 -> x4, local copies, waits for them, and re-layouts: 6.84 us -> 5.9 us
where the time goes in v2:
time: 42 us; the launch traced here: 41.8 us
  Pallas kernels  35.3 us (84%)
  local copies, waits for them, and re-layouts  5.9 us (14%)
  between operations  0.64 us (2%)
    pallas_call x1, Pallas kernels, local(): pl.pallas_call(functools.partial(kernel, count, (pols, dirs, channels, wi...  35.3 us
    unnamed x4, local copies, waits for them, and re-layouts  5.9 us

profile of v2, /device:TPU:0, one launch (start us, length us, event | category | flops | bytes accessed | tf_op | source)
XLA Modules:
  0.0 41.8 jit_solution(4381395453237006898)
XLA Ops:
  0.6 35.3 %shard_map.75 = (f32[2,2,16,4,62]{4,3,2,1,0:T(4,128)}, f32[2,2,16,4,62]{4,3,2,1,0:T(4,128)}, f32[2,2,16,4,62]{4,3,2,1,0:T(4,128)}, f32[2,2]{1,0:T(2,128)}) custom-call(f32[2,2,4,1,3844]{4,3,2,1,0:T(1,128)} %vis_in.1, bf16[2,2,16,4,3844]{4,3,2,1,0:T(4,128)(2,1)} %bitcast.1, f32[2,2,16,4,62]{4,3,2,1,0:T(4,128)} %jones_in.1, f32[2,2,16,4,62]{4,3,2,1,0:T(4,128)} %duals_in.1), custom_call_target="tpu_custom_call" | custom-call | tf_op jit(solution)/shard_map/pallas_call | solution.py:322
  35.9 1.6 %copy.12 = f32[2,2,16,4,62]{4,3,2,1,0:T(4,128)} copy(f32[2,2,16,4,62]{4,3,2,1,0:T(4,128)} %get-tuple-element.8) | data formatting | bytes 126976
  37.5 1.6 %copy.13 = f32[2,2,16,4,62]{4,3,2,1,0:T(4,128)} copy(f32[2,2,16,4,62]{4,3,2,1,0:T(4,128)} %get-tuple-element.9) | data formatting | bytes 126976
  39.0 1.6 %copy.14 = f32[2,2,16,4,62]{4,3,2,1,0:T(4,128)} copy(f32[2,2,16,4,62]{4,3,2,1,0:T(4,128)} %get-tuple-element.10) | data formatting | bytes 126976
  40.6 1.2 %copy.15 = f32[2,2]{1,0:T(2,128)} copy(f32[2,2]{1,0:T(2,128)} %get-tuple-element.11) | data formatting | bytes 32

commit v3 on v2

--- a/solution.py
+++ b/solution.py
@@ -10,7 +10,6 @@
 ITERS = 2
 HALF = 64
 BLOCK = 256
-UNROLL = 2
 MESH = pl.DeviceIdType.MESH
 
 penalty = 8.0
@@ -30,8 +29,10 @@
         first = jnp.floor((pair + 0.5) * (1.0 / width))
         second = pair - first * width
         keep = (first != second) & (first < width)
-        spread_p[:, pl.ds(start, BLOCK)] = jnp.where((first == station) & keep, 1.0, 0.0).astype(jnp.bfloat16)
-        spread_q[:, pl.ds(start, BLOCK)] = jnp.where((second == station) & keep, 1.0, 0.0).astype(jnp.bfloat16)
+        for table, which in ((spread_p, first), (spread_q, second)):
+            chosen = jnp.where((which == station) & keep, 1.0, 0.0).astype(jnp.bfloat16)
+            table[0:HALF, pl.ds(start, BLOCK)] = chosen
+            table[HALF:, pl.ds(start, BLOCK)] = chosen
         pair = (lax.broadcasted_iota(jnp.int32, (BLOCK, 2 * HALF), 0) + start).astype(jnp.float32)
         station = (lax.broadcasted_iota(jnp.int32, (BLOCK, 2 * HALF), 1) & (HALF - 1)).astype(jnp.float32)
         inside = pair - station * width
@@ -48,7 +49,7 @@
     jones_out, consensus_out, duals_out, norms_out,
     vis_raw, sky_raw, jones_raw, duals_raw,
     vis, sky, spread_p, spread_q, gather_p, lhs, left, right, parts,
-    gain, cons, dual, total, summed, from_low, from_high, sums, slots,
+    gain, cons, dual, summed, from_low, from_high, sums, slots,
     load_sem, sky_sem, send_sem, low_sem, high_sem, norm_send, norm_recv,
 ):
     pols, dirs, channels, width, pairs, blocks, entries = dims
@@ -111,24 +112,17 @@
 
     def solve(pol):
         now = gain[pol].reshape(tall, 128)
-        high, low = split(now)
-        lhs[pol, 0:tall, 0:128] = high
-        lhs[pol, 0:tall, 128:256] = low
-        high, low = split(pltpu.roll(now, HALF, 1))
-        lhs[pol, tall:, 0:128] = high
-        lhs[pol, tall:, 128:256] = low
-        total[...] = jnp.zeros_like(total)
-
-        def one_block(start, u):
-            zeros = jnp.zeros((HALF, BLOCK), jnp.bfloat16)
-            ep = spread_p[:, pl.ds(start, BLOCK)]
-            eq = spread_q[:, pl.ds(start, BLOCK)]
-            gains = lhs[pol]
-            left[u] = jnp.dot(gains, jnp.concatenate([ep, zeros, ep, zeros], 0), preferred_element_type=jnp.float32)
-            right[u] = jnp.dot(gains, jnp.concatenate([eq, zeros, eq, zeros], 0), preferred_element_type=jnp.float32)
-            for lane in range(0, BLOCK, 128):
-                lanes = pl.ds(pl.multiple_of(start + lane, 128), 128)
-                here = slice(lane, lane + 128)
+        lane = lax.broadcasted_iota(jnp.int32, (tall, 128), 1)
+        high = now.astype(jnp.bfloat16).astype(jnp.float32)
+        low = now - high
+        lhs[pol, 0:tall] = jnp.where(lane < HALF, high, pltpu.roll(low, HALF, 1)).astype(jnp.bfloat16)
+        lhs[pol, tall:] = jnp.where(lane < HALF, pltpu.roll(high, HALF, 1), low).astype(jnp.bfloat16)
+        right[...] = jnp.dot(lhs[pol], spread_q[...], preferred_element_type=jnp.float32)
+        left[...] = jnp.dot(lhs[pol], spread_p[...], preferred_element_type=jnp.float32)
+
+        def one_block(b, carry):
+            for sub in range(0, BLOCK, 128):
+                lanes = pl.ds(pl.multiple_of(b * BLOCK + sub, 128), 128)
                 model_r = jnp.zeros((8, 128), jnp.float32)
                 model_i = jnp.zeros((8, 128), jnp.float32)
                 held = []
@@ -136,8 +130,8 @@
                     sr, si = sky[0, pol, t, :, lanes], sky[1, pol, t, :, lanes]
                     mine = slice(t * 8, (t + 1) * 8)
                     other = slice(tall + t * 8, tall + (t + 1) * 8)
-                    rr, ri = right[u, mine, here], right[u, other, here]
-                    lr, li = left[u, mine, here], left[u, other, here]
+                    rr, ri = right[mine, lanes], right[other, lanes]
+                    lr, li = left[mine, lanes], left[other, lanes]
                     zr = sr * rr + si * ri
                     zi = sr * ri - si * rr
                     model_r = model_r + (lr * zr + li * zi)
@@ -157,27 +151,15 @@
                         [zr * zr + zi * zi for zr, zi in pair],
                     )
                     for i, value in enumerate(values):
-                        high, low = split(jnp.concatenate(value, 0))
-                        at = slice(i * tall + t * 8, i * tall + (t + 2) * 8)
-                        parts[u, 0, at, here] = high
-                        parts[u, 1, at, here] = low
-            weight = gather_p[pl.ds(start, BLOCK), :]
-            return jnp.dot(parts[u, 0], weight, preferred_element_type=jnp.float32) + jnp.dot(
-                parts[u, 1], weight, preferred_element_type=jnp.float32
-            )
-
-        def several(b, carry):
-            added = None
-            for u in range(UNROLL):
-                start = pl.multiple_of((b * UNROLL + u) * BLOCK, BLOCK)
-                term = one_block(start, u)
-                added = term if added is None else added + term
-            total[...] += added
+                        upper, rest = split(jnp.concatenate(value, 0))
+                        parts[i * tall + t * 8 : i * tall + (t + 2) * 8, lanes] = upper
+                        parts[(3 + i) * tall + t * 8 : (3 + i) * tall + (t + 2) * 8, lanes] = rest
             return carry
 
-        lax.fori_loop(0, blocks // UNROLL, several, 0)
-
-        lane = lax.broadcasted_iota(jnp.int32, (tall, 128), 1)
+        lax.fori_loop(0, blocks, one_block, 0)
+
+        both = jnp.dot(parts[...], gather_p[...], preferred_element_type=jnp.float32)
+        total = both[0 : 3 * tall] + both[3 * tall :]
         upper = jnp.where(lane < HALF, total[0:tall], total[tall : 2 * tall]).reshape(tiles, 8, 128)
         lower = total[2 * tall :].reshape(tiles, 8, 128)
         fresh = (upper + gain[pol] * lower + penalty * (cons[pol] - dual[pol])) / (lower + penalty)
@@ -310,7 +292,7 @@
         pairs = visibility.shape[-1]
         times = visibility.shape[3]
         assert times == 1 and channels == 4 and dirs % 4 == 0 and width <= HALF - 2
-        blocks = pl.cdiv(pairs, BLOCK * UNROLL) * UNROLL
+        blocks = pl.cdiv(pairs, BLOCK)
         long = blocks * BLOCK
         tiles = dirs * channels // 8
         tall = tiles * 8
@@ -331,17 +313,16 @@
                 pltpu.VMEM(duals_start.shape, f32),
                 pltpu.VMEM((2, pols, 8, long), f32),
                 pltpu.VMEM((2, pols, tiles, 8, long), f32),
-                pltpu.VMEM((HALF, long), bf16),
-                pltpu.VMEM((HALF, long), bf16),
+                pltpu.VMEM((2 * HALF, long), bf16),
+                pltpu.VMEM((2 * HALF, long), bf16),
                 pltpu.VMEM((long, 2 * HALF), bf16),
-                pltpu.VMEM((pols, 2 * tall, 4 * HALF), bf16),
-                pltpu.VMEM((UNROLL, 2 * tall, BLOCK), f32),
-                pltpu.VMEM((UNROLL, 2 * tall, BLOCK), f32),
-                pltpu.VMEM((UNROLL, 2, 3 * tall, BLOCK), bf16),
+                pltpu.VMEM((pols, 2 * tall, 2 * HALF), bf16),
+                pltpu.VMEM((2 * tall, long), f32),
+                pltpu.VMEM((2 * tall, long), f32),
+                pltpu.VMEM((6 * tall, long), bf16),
                 pltpu.VMEM(packed, f32),
                 pltpu.VMEM(packed, f32),
                 pltpu.VMEM(packed, f32),
-                pltpu.VMEM((3 * tall, 2 * HALF), f32),
                 pltpu.VMEM((ITERS,) + packed, f32),
                 pltpu.VMEM((ITERS,) + packed, f32),
                 pltpu.VMEM((ITERS,) + packed, f32),

time: 42 us -> 40.2 us (0.957)
  Pallas kernels: 35.3 us -> 33.5 us
    pallas_call x1, Pallas kernels: 35.3 us -> 33.5 us  [local(): pl.pallas_call(functools.partial(kernel, count, (pols, dirs, channels, wi...]
where the time goes in v3:
time: 40.2 us; the launch traced here: 40 us
  Pallas kernels  33.5 us (83%)
  local copies, waits for them, and re-layouts  5.9 us (15%)
  between operations  0.64 us (2%)
    pallas_call x1, Pallas kernels, local(): pl.pallas_call(functools.partial(kernel, count, (pols, dirs, channels, wi...  33.5 us
    unnamed x4, local copies, waits for them, and re-layouts  5.9 us

profile of v3, /device:TPU:0, one launch (start us, length us, event | category | flops | bytes accessed | tf_op | source)
XLA Modules:
  0.0 40.0 jit_solution(9420234406341352010)
XLA Ops:
  0.6 33.5 %shard_map.75 = (f32[2,2,16,4,62]{4,3,2,1,0:T(4,128)}, f32[2,2,16,4,62]{4,3,2,1,0:T(4,128)}, f32[2,2,16,4,62]{4,3,2,1,0:T(4,128)}, f32[2,2]{1,0:T(2,128)}) custom-call(f32[2,2,4,1,3844]{4,3,2,1,0:T(1,128)} %vis_in.1, bf16[2,2,16,4,3844]{4,3,2,1,0:T(4,128)(2,1)} %bitcast.1, f32[2,2,16,4,62]{4,3,2,1,0:T(4,128)} %jones_in.1, f32[2,2,16,4,62]{4,3,2,1,0:T(4,128)} %duals_in.1), custom_call_target="tpu_custom_call" | custom-call | tf_op jit(solution)/shard_map/pallas_call | solution.py:304
  34.1 1.6 %copy.12 = f32[2,2,16,4,62]{4,3,2,1,0:T(4,128)} copy(f32[2,2,16,4,62]{4,3,2,1,0:T(4,128)} %get-tuple-element.8) | data formatting | bytes 126976
  35.7 1.6 %copy.13 = f32[2,2,16,4,62]{4,3,2,1,0:T(4,128)} copy(f32[2,2,16,4,62]{4,3,2,1,0:T(4,128)} %get-tuple-element.9) | data formatting | bytes 126976
  37.2 1.6 %copy.14 = f32[2,2,16,4,62]{4,3,2,1,0:T(4,128)} copy(f32[2,2,16,4,62]{4,3,2,1,0:T(4,128)} %get-tuple-element.10) | data formatting | bytes 126976
  38.8 1.2 %copy.15 = f32[2,2]{1,0:T(2,128)} copy(f32[2,2]{1,0:T(2,128)} %get-tuple-element.11) | data formatting | bytes 32
